TPU v7x, 32 devices: a whole 2x2x4 slice. The times are simulated.
32 devices in a mesh: member: 4 (over y, x), dom: 8 (over z, core).
Axes of the slice: x: 2, y: 2, z: 4, core: 2. Of those that a mesh axis runs over, the one named last changes fastest.
Arguments:
- acoustic_perturbation: float32 [4, 32, 8192], P('member', None, 'dom'), may hold values from -8 to 8
- prior_acoustic_state: float32 [4, 32, 8192], P('member', None, 'dom'), may hold values from -8 to 8
- thermal_anomaly: float32 [4, 32, 8192], P('member', None, 'dom'), may hold values from -8 to 8
- model_parameters: float32 [4, 4], P('member'), may hold values from 0.5 to 1.5
- crossing_velocity: float32 [32, 24576], P(None, 'dom'), may hold values from -3 to 3
- face_extent: float32 [24576], P('dom'), may hold values from 0.1 to 0.4
- face_metric_factor: float32 [24576], P('dom'), may hold values from 0.01 to 0.06
- reciprocal_polygon_surface: float32 [8192], P('dom'), may hold values from 0.5 to 2
- owned_totals: int32 [8], P('dom'), may hold values from 768 to 1024, as said below
- export_lists: int32 [8, 6, 128], P('dom'), may hold values from 0 to 1024, as said below
- face_neighbour_pair: int32 [2, 24576], P(None, 'dom'), may hold values from 0 to 1792, as said below
- polygon_side_lookup: int32 [6, 8192], P(None, 'dom'), may hold values from 0 to 3072, as said below
Outputs:
- pressure_out: float32 [4, 32, 8192], P('member', None, 'dom')
- temperature_out: float32 [4, 32, 8192], P('member', None, 'dom')
- ensemble_mean: float32 [32, 8192], P(None, 'dom')
Inputs may be any that keep to these rules, and one draw needn't show every extreme that they name: The first owned_totals[p] cell slots of partition p are its cells, the rest unused; some partition has 1024. Row export_lists[p, b] lists owned cells of partition p sent to partition (p + offsets[b]) mod 8; filled entries first, then 1024 in the empty slots; at least 64 filled entries a row; in every draw some partition receives 128 filled entries in all 6 of its rows. `face_neighbour_pair`: edge 3 i + j of partition p starts at owned cell i and ends at another owned cell or at halo column 1024 + b * 128 + k whose slot k is filled in the sender's row b; edges of unused cells have both ends at 1792. `polygon_side_lookup`: the local edges with an end at each owned cell, 3072 in empty slots; unused cells have only empty slots.
All inputs are finite; a program needn't handle non-finite values.
Results may differ from a plain program's by a relative error of at most 0.0001.
Values sent between devices are 32-bit elements; how exact they have to be, the bound alone decides.
A program may use at most 64 MiB of HBM per device.

v0:
```python
import math

import jax
import jax.numpy as jnp
from jax import lax
from jax.sharding import PartitionSpec as P

STEPS = 2
NS = 3


time_step = 0.25


def passed_along(block, axis, distance):
    devices = range(lax.axis_size(axis))
    route = [((i - distance) % len(devices), i) for i in devices]
    return lax.ppermute(block, axis, route)


def neighbour_offsets(count):
    return [(block_number // 2 + 1) * (1 - 2 * (block_number % 2)) for block_number in range(count)]


def exact_dot(left_side, right_side):
    return jnp.dot(
        left_side, right_side, precision=lax.Precision.HIGHEST, preferred_element_type=jnp.float32
    )


def edge_block_size(edge_count):
    return math.gcd(edge_count, 384)


def gather_ends(extended, finish):
    edge_count = finish.shape[0]
    block_size = edge_block_size(edge_count)
    column_count = extended.shape[1]
    index_blocks = finish.reshape(edge_count // block_size, block_size)

    def one_block(indices):
        selector = (
            lax.broadcasted_iota(jnp.int32, (column_count, block_size), 0) == indices[None, :]
        ).astype(jnp.float32)
        return exact_dot(extended, selector)

    blocks = lax.map(one_block, index_blocks)
    return jnp.transpose(blocks, (1, 0, 2)).reshape(extended.shape[0], edge_count)


def divergence(fluxes, finish, cell_count):
    levels = fluxes.shape[0]
    edge_count = fluxes.shape[1]
    block_size = edge_block_size(edge_count)
    block_count = edge_count // block_size
    index_blocks = finish.reshape(block_count, block_size)
    flux_blocks = jnp.transpose(fluxes.reshape(levels, block_count, block_size), (1, 0, 2))

    def add_block(total, items):
        indices, flux_piece = items
        selector = (
            indices[:, None] == lax.broadcasted_iota(jnp.int32, (block_size, cell_count), 1)
        ).astype(jnp.float32)
        return (total + exact_dot(flux_piece, selector), None)

    incoming, unused = lax.scan(
        add_block, jnp.zeros((levels, cell_count), jnp.float32), (index_blocks, flux_blocks)
    )
    outgoing = jnp.sum(fluxes.reshape(levels, cell_count, 3), axis=2)
    return outgoing - incoming


def outgoing_rows(fields, export_lists):
    listed = export_lists[0].reshape(-1)
    selector = (
        lax.broadcasted_iota(jnp.int32, (fields.shape[1], listed.shape[0]), 0) == listed[None, :]
    ).astype(jnp.float32)
    chosen = exact_dot(fields, selector)
    zero_column = jnp.zeros((fields.shape[0], 1), jnp.float32)
    return (
        chosen.reshape(fields.shape[0], export_lists.shape[1], export_lists.shape[2]),
        zero_column,
    )


def extend(fields, export_lists):
    outgoing, zero_column = outgoing_rows(fields, export_lists)
    dom_count = lax.axis_size("dom")
    pieces = []
    for block_number, offset in enumerate(neighbour_offsets(export_lists.shape[1])):
        pieces.append(passed_along(outgoing[:, block_number], "dom", offset % dom_count))
    return jnp.concatenate([fields] + pieces + [zero_column], axis=1)


def starts_of(fields):
    levels = fields.shape[0]
    cell_count = fields.shape[1]
    return jnp.broadcast_to(fields[:, :, None], (levels, cell_count, 3)).reshape(
        levels, 3 * cell_count
    )


def per_device(
    acoustic_perturbation,
    prior_acoustic_state,
    thermal_anomaly,
    model_parameters,
    crossing_velocity,
    face_extent,
    face_metric_factor,
    reciprocal_polygon_surface,
    owned_totals,
    export_lists,
    face_neighbour_pair,
    polygon_side_lookup,
):
    levels = acoustic_perturbation.shape[1]
    cell_count = acoustic_perturbation.shape[2]
    current = acoustic_perturbation[0]
    previous = prior_acoustic_state[0]
    scalar_quantity = thermal_anomaly[0]
    speed = model_parameters[0, 0]
    kappa = 0.5 * model_parameters[0, 1]
    mixing = 0.6 * model_parameters[0, 2]
    couple = model_parameters[0, 3]
    owned = (jnp.arange(cell_count, dtype=jnp.int32) < owned_totals[0])[None, :]
    cell_area = jnp.where(owned[0], 1.0 / reciprocal_polygon_surface, 0.0)
    finish = face_neighbour_pair[1]
    inverse = reciprocal_polygon_surface[None, :]
    for outer_step in range(STEPS):
        extended = extend(jnp.concatenate([scalar_quantity, current], axis=0), export_lists)
        theta_ext = extended[:levels]
        press_ext = extended[levels:]
        left = starts_of(scalar_quantity)
        right = gather_ends(theta_ext, finish)
        fluxes = face_extent[None, :] * (
            0.5 * crossing_velocity * (left + right)
            - (0.5 * jnp.abs(crossing_velocity) + kappa) * (right - left)
        )
        differences = scalar_quantity[1:] - scalar_quantity[:-1]
        zero_row = jnp.zeros((1, cell_count), jnp.float32)
        vertical = mixing * (
            jnp.concatenate([differences, zero_row], 0)
            - jnp.concatenate([zero_row, differences], 0)
        )
        advanced = jnp.where(
            owned,
            scalar_quantity
            + time_step * (-inverse * divergence(fluxes, finish, cell_count) + vertical),
            scalar_quantity,
        )
        forcing = couple * (advanced - scalar_quantity) / NS
        for substep in range(NS):
            if substep > 0:
                press_ext = extend(current, export_lists)
            gradient = face_metric_factor[None, :] * (
                gather_ends(press_ext, finish) - starts_of(current)
            )
            stepped = jnp.where(
                owned,
                2.0 * current
                - previous
                + speed * inverse * divergence(gradient, finish, cell_count)
                + forcing,
                current,
            )
            previous, current = (current, stepped)
        weighted, area_total = lax.psum(
            (jnp.sum(current * cell_area[None, :], axis=1), jnp.sum(cell_area)), "dom"
        )
        level_mean = (weighted / area_total)[:, None]
        current = jnp.where(owned, current - level_mean, current)
        previous = jnp.where(owned, previous - level_mean, previous)
        scalar_quantity = advanced
    ensemble = lax.psum(current, "member") / lax.axis_size("member")
    return (current[None], scalar_quantity[None], ensemble)


def solution(mesh):
    in_specs = (
        P("member", None, "dom"),
        P("member", None, "dom"),
        P("member", None, "dom"),
        P("member", None),
        P(None, "dom"),
        P("dom"),
        P("dom"),
        P("dom"),
        P("dom"),
        P("dom", None, None),
        P(None, "dom"),
        P(None, "dom"),
    )
    out_specs = (P("member", None, "dom"), P("member", None, "dom"), P(None, "dom"))
    return jax.shard_map(
        per_device, mesh=mesh, in_specs=in_specs, out_specs=out_specs, check_vma=False
    )
```

profile of v0, /device:TPU:0, one launch (start us, length us, event | category | flops | bytes accessed | tf_op | source)
XLA Modules:
  0.0 611.1 jit_solution(15316306464230908391)
XLA Ops:
  10.1 2.8 fusion.79
  14.2 4.0 collective-permute-start.1
  18.5 3.5 collective-permute-start.3
  30.6 3.8 reshape.204
  42.2 3.2 collective-permute-start.5
  58.3 9.1 %while.168 = (s32[]{:T(128)}, f32[8,32,384]{2,1,0:T(8,128)S(1)}, s32[8,384]{1,0:T(8,128)S(1)}, f32[32,1793]{1,0:T(8,128)S(1)}, s32[]{:T(128)}) while((s32[]{:T(128)}, f32[8,32,384]{2,1,0:T(8,128)S(1)}, s32[8,384]{1,0:T(8,128)S(1)}, f32[32,1793]{1,0:T(8,128)S(1)}, s32[]{:T(128)}) %tuple.345), condition=%wide.region_1.2_spmd, body=%wide.region_0.1_spmd.sunk | while | flops 265077120 | bytes 300101 | solution.py:47
  67.8 3.0 multiply_bitcast_fusion.5
  72.7 23.0 %while.176 = (s32[]{:T(128)}, f32[32,1024]{1,0:T(8,128)}, f32[8,32,384]{2,1,0:T(8,128)S(1)}, s32[8,384]{1,0:T(8,128)S(1)}, s32[]{:T(128)}, /*index=5*/s32[]{:T(128)}) while((s32[]{:T(128)}, f32[32,1024]{1,0:T(8,128)}, f32[8,32,384]{2,1,0:T(8,128)S(1)}, s32[8,384]{1,0:T(8,128)S(1)}, s32[]{:T(128)}, /*index=5*/s32[]{:T(128)}) %tuple.395), condition=%wide.region_4.5_spmd.clone, body=%wide.region_3.4_spmd.clone.sunk | while | flops 151453696 | bytes 315991 | solution.py:66
  99.7 16.6 %while.169 = (s32[]{:T(128)}, f32[8,32,384]{2,1,0:T(8,128)S(1)}, s32[8,384]{1,0:T(8,128)S(1)}, f32[32,1793]{1,0:T(8,128)}, s32[]{:T(128)}) while((s32[]{:T(128)}, f32[8,32,384]{2,1,0:T(8,128)S(1)}, s32[8,384]{1,0:T(8,128)S(1)}, f32[32,1793]{1,0:T(8,128)}, s32[]{:T(128)}) %tuple.396), condition=%wide.region_6.7_spmd, body=%wide.region_5.6_spmd.sunk | while | flops 265077120 | bytes 283845 | solution.py:47
  120.1 25.9 %while.177 = (s32[]{:T(128)}, f32[32,1024]{1,0:T(8,128)}, f32[8,32,384]{2,0,1:T(8,128)}, s32[8,384]{1,0:T(8,128)S(1)}, s32[]{:T(128)}, /*index=5*/s32[]{:T(128)}) while((s32[]{:T(128)}, f32[32,1024]{1,0:T(8,128)}, f32[8,32,384]{2,0,1:T(8,128)}, s32[8,384]{1,0:T(8,128)S(1)}, s32[]{:T(128)}, /*index=5*/s32[]{:T(128)}) %tuple.410), condition=%wide.region_9.10_spmd.clone, body=%wide.region_8.9_spmd.clone.sunk | while | flops 151453696 | bytes 414295 | solution.py:66
  149.7 3.7 reshape.207
  153.4 7.6 %multiply_reduce_fusion.5 = f32[32,1024]{0,1:T(8,128)} fusion(f32[32,1024,3]{0,2,1:T(4,128)} %reshape.203, f32[32,1024]{0,1:T(8,128)S(1)} %bitcast.284, f32[1024,3]{1,0:T(8,128)S(1)} %mul.239), kind=kLoop, calls=%fused_computation.122 | loop fusion | flops 262144 | bytes 667648 | tf_op jit(solution)/shard_map/reduce_sum | solution.py:69
  161.0 3.7 reduce_sum.104
  164.7 3.5 fusion.93
  169.6 3.7 collective-permute-start.7
  175.0 3.8 collective-permute-start.9
  180.5 3.8 reshape.211
  186.0 3.8 reshape.218
  199.4 16.6 %while.170 = (s32[]{:T(128)}, f32[8,32,384]{2,1,0:T(8,128)S(1)}, s32[8,384]{1,0:T(8,128)S(1)}, f32[32,1793]{1,0:T(8,128)}, s32[]{:T(128)}) while((s32[]{:T(128)}, f32[8,32,384]{2,1,0:T(8,128)S(1)}, s32[8,384]{1,0:T(8,128)S(1)}, f32[32,1793]{1,0:T(8,128)}, s32[]{:T(128)}) %tuple.398), condition=%wide.region_11.12_spmd, body=%wide.region_10.11_spmd.sunk | while | flops 265077120 | bytes 283845 | solution.py:47
  217.6 3.5 multiply_bitcast_fusion.4
  223.0 6.2 %while.178 = (s32[]{:T(128)}, f32[32,1024]{1,0:T(8,128)S(1)}, f32[8,32,384]{2,1,0:T(8,128)S(1)}, s32[8,384]{1,0:T(8,128)S(1)}, s32[]{:T(128)}, /*index=5*/s32[]{:T(128)}) while((s32[]{:T(128)}, f32[32,1024]{1,0:T(8,128)S(1)}, f32[8,32,384]{2,1,0:T(8,128)S(1)}, s32[8,384]{1,0:T(8,128)S(1)}, s32[]{:T(128)}, ...), condition=%wide.region_14.15_spmd.clone, body=%wide.region_13.14_spmd.clone.sunk | while | flops 151453696 | bytes 316503 | solution.py:66
  230.3 3.7 reshape.210
  233.9 6.9 %multiply_reduce_fusion.4 = f32[32,1024]{0,1:T(8,128)S(1)} fusion(f32[32,1024,3]{0,2,1:T(4,128)} %reshape.210, f32[32,1024]{0,1:T(8,128)S(1)} %get-tuple-element.831, f32[1024,3]{1,0:T(8,128)S(1)} %mul.239), kind=kLoop, calls=%fused_computation.121 | loop fusion | flops 262144 | bytes 667648 | tf_op jit(solution)/shard_map/reduce_sum | solution.py:69
  242.7 3.6 collective-permute-start.13
  246.3 3.8 collective-permute-start.15
  251.8 3.8 reshape.214
  255.7 2.8 collective-permute-start.17
  260.0 9.0 %while.171 = (s32[]{:T(128)}, f32[8,32,384]{2,1,0:T(8,128)S(1)}, s32[8,384]{1,0:T(8,128)S(1)}, f32[32,1793]{1,0:T(8,128)S(1)}, s32[]{:T(128)}) while((s32[]{:T(128)}, f32[8,32,384]{2,1,0:T(8,128)S(1)}, s32[8,384]{1,0:T(8,128)S(1)}, f32[32,1793]{1,0:T(8,128)S(1)}, s32[]{:T(128)}) %tuple.400), condition=%wide.region_16.17_spmd, body=%wide.region_15.16_spmd.sunk | while | flops 265077120 | bytes 300101 | solution.py:47
  270.7 3.5 multiply_bitcast_fusion.3
  276.1 6.2 %while.179 = (s32[]{:T(128)}, f32[32,1024]{1,0:T(8,128)S(1)}, f32[8,32,384]{2,1,0:T(8,128)S(1)}, s32[8,384]{1,0:T(8,128)S(1)}, s32[]{:T(128)}, /*index=5*/s32[]{:T(128)}) while((s32[]{:T(128)}, f32[32,1024]{1,0:T(8,128)S(1)}, f32[8,32,384]{2,1,0:T(8,128)S(1)}, s32[8,384]{1,0:T(8,128)S(1)}, s32[]{:T(128)}, ...), condition=%wide.region_19.20_spmd.clone, body=%wide.region_18.19_spmd.clone.sunk | while | flops 151453696 | bytes 316503 | solution.py:66
  283.3 3.7 reshape.213
  287.0 6.9 %multiply_reduce_fusion.3 = f32[32,1024]{0,1:T(8,128)S(1)} fusion(f32[32,1024,3]{0,2,1:T(4,128)} %reshape.213, f32[32,1024]{0,1:T(8,128)S(1)} %add_select_fusion.5, f32[1024,3]{1,0:T(8,128)S(1)} %mul.239), kind=kLoop, calls=%fused_computation.120 | loop fusion | flops 262144 | bytes 667648 | tf_op jit(solution)/shard_map/reduce_sum | solution.py:69
  294.9 14.8 %all-reduce.4 = (f32[32]{0:T(128)S(1)}, f32[]{:T(128)}) all-reduce(f32[32]{0:T(128)S(1)} %get-tuple-element.829, f32[]{:T(128)} %get-tuple-element.876), channel_id=1, replica_groups=mesh['member'=4,'dom'=8] {'dom'}, use_global_device_ids=true, to_apply=%region_21.22 | all-reduce | flops 33 | bytes 264 | tf_op jit(solution)/shard_map/psum | solution.py:168
  311.1 3.5 fusion.76
  315.7 3.5 collective-permute-start.19
  319.2 3.8 collective-permute-start.21
  324.7 3.8 reshape.217
  336.2 3.0 fusion.99
  341.5 17.0 %while.173 = (s32[]{:T(128)}, f32[8,32,384]{2,1,0:T(8,128)S(1)}, s32[8,384]{1,0:T(8,128)S(1)}, f32[32,1793]{1,0:T(8,128)}, s32[]{:T(128)}) while((s32[]{:T(128)}, f32[8,32,384]{2,1,0:T(8,128)S(1)}, s32[8,384]{1,0:T(8,128)S(1)}, f32[32,1793]{1,0:T(8,128)}, s32[]{:T(128)}) %tuple.402), condition=%wide.region_30.31_spmd, body=%wide.region_29.30_spmd.sunk | while | flops 265077120 | bytes 283845 | solution.py:47
  361.4 3.7 reshape.220
  365.9 14.6 %while.181 = (s32[]{:T(128)}, f32[32,1024]{1,0:T(8,128)S(1)}, f32[8,32,384]{2,0,1:T(8,128)}, s32[8,384]{1,0:T(8,128)S(1)}, s32[]{:T(128)}, /*index=5*/s32[]{:T(128)}) while((s32[]{:T(128)}, f32[32,1024]{1,0:T(8,128)S(1)}, f32[8,32,384]{2,0,1:T(8,128)}, s32[8,384]{1,0:T(8,128)S(1)}, s32[]{:T(128)}, /*index=5*/s32[]{:T(128)}) %tuple.414), condition=%wide.region_33.34_spmd.clone, body=%wide.region_32.33_spmd.clone.sunk | while | flops 151453696 | bytes 414295 | solution.py:66
  383.0 9.1 %while.172 = (s32[]{:T(128)}, f32[8,32,384]{2,1,0:T(8,128)S(1)}, s32[8,384]{1,0:T(8,128)S(1)}, f32[32,1793]{1,0:T(8,128)S(1)}, s32[]{:T(128)}) while((s32[]{:T(128)}, f32[8,32,384]{2,1,0:T(8,128)S(1)}, s32[8,384]{1,0:T(8,128)S(1)}, f32[32,1793]{1,0:T(8,128)S(1)}, s32[]{:T(128)}) %tuple.404), condition=%wide.region_25.26_spmd, body=%wide.region_24.25_spmd.sunk | while | flops 265077120 | bytes 300101 | solution.py:47
  393.8 3.5 multiply_bitcast_fusion.2
  399.1 6.2 %while.180 = (s32[]{:T(128)}, f32[32,1024]{1,0:T(8,128)S(1)}, f32[8,32,384]{2,1,0:T(8,128)S(1)}, s32[8,384]{1,0:T(8,128)S(1)}, s32[]{:T(128)}, /*index=5*/s32[]{:T(128)}) while((s32[]{:T(128)}, f32[32,1024]{1,0:T(8,128)S(1)}, f32[8,32,384]{2,1,0:T(8,128)S(1)}, s32[8,384]{1,0:T(8,128)S(1)}, s32[]{:T(128)}, ...), condition=%wide.region_28.29_spmd.clone, body=%wide.region_27.28_spmd.clone.sunk | while | flops 151453696 | bytes 316503 | solution.py:66
  406.4 3.7 reshape.216
  410.1 7.6 %multiply_reduce_fusion.2 = f32[32,1024]{0,1:T(8,128)} fusion(f32[32,1024,3]{0,2,1:T(4,128)} %reshape.216, f32[32,1024]{0,1:T(8,128)S(1)} %subtract_select_fusion.2, f32[1024,3]{1,0:T(8,128)S(1)} %mul.239), kind=kLoop, calls=%fused_computation.119 | loop fusion | flops 262144 | bytes 667648 | tf_op jit(solution)/shard_map/reduce_sum | solution.py:69
  417.8 3.8 reduce_sum.110
  421.6 3.6 fusion.89
  427.2 3.5 collective-permute-start.25
  430.7 3.8 collective-permute-start.27
  443.5 9.1 %while.174 = (s32[]{:T(128)}, f32[8,32,384]{2,1,0:T(8,128)S(1)}, s32[8,384]{1,0:T(8,128)S(1)}, f32[32,1793]{1,0:T(8,128)S(1)}, s32[]{:T(128)}) while((s32[]{:T(128)}, f32[8,32,384]{2,1,0:T(8,128)S(1)}, s32[8,384]{1,0:T(8,128)S(1)}, f32[32,1793]{1,0:T(8,128)S(1)}, s32[]{:T(128)}) %tuple.406), condition=%wide.region_35.36_spmd, body=%wide.region_34.35_spmd.sunk | while | flops 265077120 | bytes 300101 | solution.py:47
  453.1 3.1 multiply_bitcast_fusion.1
  458.0 6.2 %while.182 = (s32[]{:T(128)}, f32[32,1024]{1,0:T(8,128)S(1)}, f32[8,32,384]{2,1,0:T(8,128)S(1)}, s32[8,384]{1,0:T(8,128)S(1)}, s32[]{:T(128)}, /*index=5*/s32[]{:T(128)}) while((s32[]{:T(128)}, f32[32,1024]{1,0:T(8,128)S(1)}, f32[8,32,384]{2,1,0:T(8,128)S(1)}, s32[8,384]{1,0:T(8,128)S(1)}, s32[]{:T(128)}, ...), condition=%wide.region_38.39_spmd.clone, body=%wide.region_37.38_spmd.clone.sunk | while | flops 151453696 | bytes 316503 | solution.py:66
  467.0 7.0 %multiply_reduce_fusion.1 = f32[32,1024]{0,1:T(8,128)S(1)} fusion(f32[32,1024,3]{0,2,1:T(4,128)} %reshape.223, f32[32,1024]{0,1:T(8,128)S(1)} %get-tuple-element.824, f32[1024,3]{1,0:T(8,128)S(1)} %mul.239), kind=kLoop, calls=%fused_computation.118 | loop fusion | flops 262144 | bytes 667648 | tf_op jit(solution)/shard_map/reduce_sum | solution.py:69
  475.8 3.6 collective-permute-start.31
  479.4 3.8 collective-permute-start.33
  484.9 3.8 reshape.227
  488.7 2.8 collective-permute-start.35
  493.1 9.0 %while.175 = (s32[]{:T(128)}, f32[8,32,384]{2,1,0:T(8,128)S(1)}, s32[8,384]{1,0:T(8,128)S(1)}, f32[32,1793]{1,0:T(8,128)S(1)}, s32[]{:T(128)}) while((s32[]{:T(128)}, f32[8,32,384]{2,1,0:T(8,128)S(1)}, s32[8,384]{1,0:T(8,128)S(1)}, f32[32,1793]{1,0:T(8,128)S(1)}, s32[]{:T(128)}) %tuple.408), condition=%wide.region_40.41_spmd, body=%wide.region_39.40_spmd.sunk | while | flops 265077120 | bytes 300101 | solution.py:47
  502.6 3.0 multiply_bitcast_fusion
  507.5 23.0 %while.183 = (s32[]{:T(128)}, f32[32,1024]{1,0:T(8,128)}, f32[8,32,384]{2,1,0:T(8,128)S(1)}, s32[8,384]{1,0:T(8,128)S(1)}, s32[]{:T(128)}, /*index=5*/s32[]{:T(128)}) while((s32[]{:T(128)}, f32[32,1024]{1,0:T(8,128)}, f32[8,32,384]{2,1,0:T(8,128)S(1)}, s32[8,384]{1,0:T(8,128)S(1)}, s32[]{:T(128)}, /*index=5*/s32[]{:T(128)}) %tuple.409), condition=%wide.region_43.44_spmd.clone, body=%wide.region_42.43_spmd.clone.sunk | while | flops 151453696 | bytes 315991 | solution.py:66
  534.1 6.9 %multiply_reduce_fusion = f32[32,1024]{0,1:T(8,128)S(1)} fusion(f32[32,1024,3]{0,2,1:T(4,128)} %reshape.226, f32[32,1024]{0,1:T(8,128)S(1)} %add_select_fusion.3, f32[1024,3]{1,0:T(8,128)S(1)} %mul.239), kind=kLoop, calls=%fused_computation.117 | loop fusion | flops 262144 | bytes 667648 | tf_op jit(solution)/shard_map/reduce_sum | solution.py:69
  541.9 14.2 %psum.33 = f32[32]{0:T(128)S(1)} all-reduce(f32[32]{0:T(128)S(1)} %get-tuple-element.822), channel_id=1, replica_groups=mesh['member'=4,'dom'=8] {'dom'}, use_global_device_ids=true, to_apply=%region_45.46 | all-reduce | flops 32 | bytes 256 | tf_op jit(solution)/shard_map/psum | solution.py:168
  558.9 43.2 %all-reduce.7.cloned.1.call-done = f32[32,1024]{0,1:T(8,128)} async-done(((f32[32,1024]{0,1:T(8,128)}), f32[32,1024]{0,1:T(8,128)}) %all-reduce.7.cloned.1.call-update) | async-done | bytes 131088 | tf_op jit(solution)/shard_map/psum | solution.py:175
  (574 shorter events, 337.2 us)
Async XLA Ops:
  7.2 594.9 %all-reduce.7.cloned.1.call-start = ((), (), s32[]{:S(2)}) async-start(), calls=%async_computation | async-start | bytes 1048576 | tf_op jit(solution)/shard_map/psum | solution.py:175
  10.1 12.9 %copy-start.35 = (s32[6,128]{1,0:T(8,128)}, s32[6,128]{1,0:T(8,128)S(1)}, u32[]{:S(2)}) copy-start(s32[6,128]{1,0:T(8,128)S(1)} %reduce.17) | copy-start | bytes 9220
  12.9 11.1 %copy-start.31 = (s32[2,3072]{1,0:T(2,128)S(1)}, s32[2,3072]{1,0:T(2,128)}, u32[]{:S(2)}) copy-start(s32[2,3072]{1,0:T(2,128)} %param.54) | copy-start | bytes 73732
  13.0 11.1 %copy-start.30 = (f32[1,4]{1,0:T(1,128)S(1)}, f32[1,4]{1,0:T(1,128)}, u32[]{:S(2)}) copy-start(f32[1,4]{1,0:T(1,128)} %param.47) | copy-start | bytes 52
  13.0 12.4 %copy-start.40 = (f32[1024]{0:T(1024)S(1)}, f32[1024]{0:T(1024)}, u32[]{:S(2)}) copy-start(f32[1024]{0:T(1024)} %param.51) | copy-start | bytes 12292
  13.0 14.9 %copy-start.25 = (f32[3072]{0:T(1024)S(1)}, f32[3072]{0:T(1024)}, u32[]{:S(2)}) copy-start(f32[3072]{0:T(1024)} %param.50) | copy-start | bytes 36868
  13.7 28.6 %collective-permute-start = (f32[64,128]{0,1:T(8,128)}, f32[64,128]{0,1:T(8,128)}, u32[]{:S(2)}, u32[]{:S(2)}) collective-permute-start(f32[64,128]{0,1:T(8,128)} %get-tuple-element.849), channel_id=1, source_target_pairs={{7,0},{0,1},{1,2},{2,3},{3,4},{4,5},{5,6},{6,7},{15,8},{8,9},{9,10... | collective-permute-start | bytes 98312 | tf_op jit(solution)/shard_map/ppermute | solution.py:18
  14.2 32.8 %collective-permute-start.1 = (f32[64,128]{0,1:T(8,128)}, f32[64,128]{0,1:T(8,128)}, u32[]{:S(2)}, u32[]{:S(2)}) collective-permute-start(f32[64,128]{0,1:T(8,128)} %get-tuple-element.848), channel_id=1, source_target_pairs={{1,0},{2,1},{3,2},{4,3},{5,4},{6,5},{7,6},{0,7},{9,8},{10,9},{11,1... | collective-permute-start | bytes 98312 | tf_op jit(solution)/shard_map/ppermute | solution.py:18
  18.2 30.2 %collective-permute-start.2 = (f32[64,128]{0,1:T(8,128)S(1)}, f32[64,128]{0,1:T(8,128)}, u32[]{:S(2)}, u32[]{:S(2)}) collective-permute-start(f32[64,128]{0,1:T(8,128)S(1)} %get-tuple-element.847), channel_id=1, source_target_pairs={{6,0},{7,1},{0,2},{1,3},{2,4},{3,5},{4,6},{5,7},{14,8},{15,9},{8,1... | collective-permute-start | bytes 98312 | tf_op jit(solution)/shard_map/ppermute | solution.py:18
  18.5 31.4 %collective-permute-start.3 = (f32[64,128]{0,1:T(8,128)S(1)}, f32[64,128]{0,1:T(8,128)}, u32[]{:S(2)}, u32[]{:S(2)}) collective-permute-start(f32[64,128]{0,1:T(8,128)S(1)} %get-tuple-element.846), channel_id=1, source_target_pairs={{2,0},{3,1},{4,2},{5,3},{6,4},{7,5},{0,6},{1,7},{10,8},{11,9},{12,... | collective-permute-start | bytes 98312 | tf_op jit(solution)/shard_map/ppermute | solution.py:18
  22.0 29.3 %collective-permute-start.4 = (f32[64,128]{0,1:T(8,128)S(1)}, f32[64,128]{0,1:T(8,128)}, u32[]{:S(2)}, u32[]{:S(2)}) collective-permute-start(f32[64,128]{0,1:T(8,128)S(1)} %get-tuple-element.845), channel_id=1, source_target_pairs={{5,0},{6,1},{7,2},{0,3},{1,4},{2,5},{3,6},{4,7},{13,8},{14,9},{15,... | collective-permute-start | bytes 98312 | tf_op jit(solution)/shard_map/ppermute | solution.py:18
  42.2 10.6 %collective-permute-start.5 = (f32[64,128]{0,1:T(8,128)S(1)}, f32[64,128]{0,1:T(8,128)S(1)}, u32[]{:S(2)}, u32[]{:S(2)}) collective-permute-start(f32[64,128]{0,1:T(8,128)S(1)} %get-tuple-element.844), channel_id=1, source_target_pairs={{3,0},{4,1},{5,2},{6,3},{7,4},{0,5},{1,6},{2,7},{11,8},{12,9},{13,... | collective-permute-start | bytes 98312 | tf_op jit(solution)/shard_map/ppermute | solution.py:18
  168.2 72.6 %copy-start.4 = (f32[32,1024]{0,1:T(8,128)}, f32[32,1024]{0,1:T(8,128)S(1)}, u32[]{:S(2)}) copy-start(f32[32,1024]{0,1:T(8,128)S(1)} %get-tuple-element.832) | copy-start | bytes 393220
  169.5 22.9 %collective-permute-start.6 = (f32[32,128]{1,0:T(8,128)S(1)}, f32[32,128]{1,0:T(8,128)S(1)}, u32[]{:S(2)}, u32[]{:S(2)}) collective-permute-start(f32[32,128]{1,0:T(8,128)S(1)} %bitcast.325), channel_id=1, source_target_pairs={{7,0},{0,1},{1,2},{2,3},{3,4},{4,5},{5,6},{6,7},{15,8},{8,9},{9,10... | collective-permute-start | bytes 49160 | tf_op jit(solution)/shard_map/ppermute | solution.py:18
  169.6 26.1 %collective-permute-start.7 = (f32[32,128]{1,0:T(8,128)S(1)}, f32[32,128]{1,0:T(8,128)S(1)}, u32[]{:S(2)}, u32[]{:S(2)}) collective-permute-start(f32[32,128]{1,0:T(8,128)S(1)} %bitcast.319), channel_id=1, source_target_pairs={{1,0},{2,1},{3,2},{4,3},{5,4},{6,5},{7,6},{0,7},{9,8},{10,9},{11,1... | collective-permute-start | bytes 49160 | tf_op jit(solution)/shard_map/ppermute | solution.py:18
  175.0 21.3 %collective-permute-start.8 = (f32[32,128]{1,0:T(8,128)S(1)}, f32[32,128]{1,0:T(8,128)S(1)}, u32[]{:S(2)}, u32[]{:S(2)}) collective-permute-start(f32[32,128]{1,0:T(8,128)S(1)} %bitcast.315), channel_id=1, source_target_pairs={{6,0},{7,1},{0,2},{1,3},{2,4},{3,5},{4,6},{5,7},{14,8},{15,9},{8,1... | collective-permute-start | bytes 49160 | tf_op jit(solution)/shard_map/ppermute | solution.py:18
  175.0 22.0 %collective-permute-start.9 = (f32[32,128]{1,0:T(8,128)S(1)}, f32[32,128]{1,0:T(8,128)S(1)}, u32[]{:S(2)}, u32[]{:S(2)}) collective-permute-start(f32[32,128]{1,0:T(8,128)S(1)} %bitcast.311), channel_id=1, source_target_pairs={{2,0},{3,1},{4,2},{5,3},{6,4},{7,5},{0,6},{1,7},{10,8},{11,9},{12,... | collective-permute-start | bytes 49160 | tf_op jit(solution)/shard_map/ppermute | solution.py:18
  178.8 18.8 %collective-permute-start.10 = (f32[32,128]{1,0:T(8,128)S(1)}, f32[32,128]{1,0:T(8,128)S(1)}, u32[]{:S(2)}, u32[]{:S(2)}) collective-permute-start(f32[32,128]{1,0:T(8,128)S(1)} %bitcast.307), channel_id=1, source_target_pairs={{5,0},{6,1},{7,2},{0,3},{1,4},{2,5},{3,6},{4,7},{13,8},{14,9},{15,... | collective-permute-start | bytes 49160 | tf_op jit(solution)/shard_map/ppermute | solution.py:18
  192.4 5.7 collective-permute-start.11
  199.4 18.2 %copy-start.12 = (f32[8,384]{1,0:T(8,128)S(1)}, f32[8,384]{1,0:T(8,128)}, u32[]{:S(2)}) copy-start(f32[8,384]{1,0:T(8,128)} %mul.242) | copy-start | bytes 36868
  217.6 5.4 copy-start.19
  233.9 6.9 %copy-start.9 = (f32[32,1024]{0,1:T(8,128)S(1)}, f32[32,1024]{0,1:T(8,128)}, u32[]{:S(2)}) copy-start(f32[32,1024]{0,1:T(8,128)} %copy.251) | copy-start | bytes 393220
  242.6 13.0 %collective-permute-start.12 = (f32[32,128]{1,0:T(8,128)S(1)}, f32[32,128]{1,0:T(8,128)S(1)}, u32[]{:S(2)}, u32[]{:S(2)}) collective-permute-start(f32[32,128]{1,0:T(8,128)S(1)} %bitcast.327), channel_id=1, source_target_pairs={{7,0},{0,1},{1,2},{2,3},{3,4},{4,5},{5,6},{6,7},{15,8},{8,9},{9,10... | collective-permute-start | bytes 49160 | tf_op jit(solution)/shard_map/ppermute | solution.py:18
  242.7 15.8 %collective-permute-start.13 = (f32[32,128]{1,0:T(8,128)S(1)}, f32[32,128]{1,0:T(8,128)S(1)}, u32[]{:S(2)}, u32[]{:S(2)}) collective-permute-start(f32[32,128]{1,0:T(8,128)S(1)} %bitcast.323), channel_id=1, source_target_pairs={{1,0},{2,1},{3,2},{4,3},{5,4},{6,5},{7,6},{0,7},{9,8},{10,9},{11,1... | collective-permute-start | bytes 49160 | tf_op jit(solution)/shard_map/ppermute | solution.py:18
  246.3 12.2 %collective-permute-start.14 = (f32[32,128]{1,0:T(8,128)S(1)}, f32[32,128]{1,0:T(8,128)S(1)}, u32[]{:S(2)}, u32[]{:S(2)}) collective-permute-start(f32[32,128]{1,0:T(8,128)S(1)} %bitcast.320), channel_id=1, source_target_pairs={{6,0},{7,1},{0,2},{1,3},{2,4},{3,5},{4,6},{5,7},{14,8},{15,9},{8,1... | collective-permute-start | bytes 49160 | tf_op jit(solution)/shard_map/ppermute | solution.py:18
  246.3 12.2 %collective-permute-start.15 = (f32[32,128]{1,0:T(8,128)S(1)}, f32[32,128]{1,0:T(8,128)S(1)}, u32[]{:S(2)}, u32[]{:S(2)}) collective-permute-start(f32[32,128]{1,0:T(8,128)S(1)} %bitcast.316), channel_id=1, source_target_pairs={{2,0},{3,1},{4,2},{5,3},{6,4},{7,5},{0,6},{1,7},{10,8},{11,9},{12,... | collective-permute-start | bytes 49160 | tf_op jit(solution)/shard_map/ppermute | solution.py:18
  250.1 8.4 %collective-permute-start.16 = (f32[32,128]{1,0:T(8,128)S(1)}, f32[32,128]{1,0:T(8,128)S(1)}, u32[]{:S(2)}, u32[]{:S(2)}) collective-permute-start(f32[32,128]{1,0:T(8,128)S(1)} %bitcast.312), channel_id=1, source_target_pairs={{5,0},{6,1},{7,2},{0,3},{1,4},{2,5},{3,6},{4,7},{13,8},{14,9},{15,... | collective-permute-start | bytes 49160 | tf_op jit(solution)/shard_map/ppermute | solution.py:18
  255.7 4.3 collective-permute-start.17
  270.7 5.4 copy-start.18
  287.0 7.0 %copy-start.5 = (f32[32,1024]{0,1:T(8,128)S(1)}, f32[32,1024]{0,1:T(8,128)}, u32[]{:S(2)}) copy-start(f32[32,1024]{0,1:T(8,128)} %copy-done.4) | copy-start | bytes 393220
  287.0 7.0 %copy-start.7 = (f32[32,1024]{0,1:T(8,128)S(1)}, f32[32,1024]{0,1:T(8,128)}, u32[]{:S(2)}) copy-start(f32[32,1024]{0,1:T(8,128)} %copy.255) | copy-start | bytes 393220
  287.0 7.0 %copy-start.26 = (f32[1024]{0:T(1024)S(1)}, f32[1024]{0:T(1024)}, u32[]{:S(2)}) copy-start(f32[1024]{0:T(1024)} %get-tuple-element.877) | copy-start | bytes 12292
  294.9 126.6 %copy-start = (f32[32,1024]{0,1:T(8,128)}, f32[32,1024]{0,1:T(8,128)S(1)}, u32[]{:S(2)}) copy-start(f32[32,1024]{0,1:T(8,128)S(1)} %get-tuple-element.830) | copy-start | bytes 393220
  314.6 14.0 %collective-permute-start.18 = (f32[64,128]{0,1:T(8,128)S(1)}, f32[64,128]{0,1:T(8,128)S(1)}, u32[]{:S(2)}, u32[]{:S(2)}) collective-permute-start(f32[64,128]{0,1:T(8,128)S(1)} %get-tuple-element.843), channel_id=1, source_target_pairs={{7,0},{0,1},{1,2},{2,3},{3,4},{4,5},{5,6},{6,7},{15,8},{8,9},{9,10... | collective-permute-start | bytes 98312 | tf_op jit(solution)/shard_map/ppermute | solution.py:18
  315.7 16.2 %collective-permute-start.19 = (f32[64,128]{0,1:T(8,128)S(1)}, f32[64,128]{0,1:T(8,128)S(1)}, u32[]{:S(2)}, u32[]{:S(2)}) collective-permute-start(f32[64,128]{0,1:T(8,128)S(1)} %get-tuple-element.842), channel_id=1, source_target_pairs={{1,0},{2,1},{3,2},{4,3},{5,4},{6,5},{7,6},{0,7},{9,8},{10,9},{11,1... | collective-permute-start | bytes 98312 | tf_op jit(solution)/shard_map/ppermute | solution.py:18
  319.2 13.2 %collective-permute-start.20 = (f32[64,128]{0,1:T(8,128)S(1)}, f32[64,128]{0,1:T(8,128)S(1)}, u32[]{:S(2)}, u32[]{:S(2)}) collective-permute-start(f32[64,128]{0,1:T(8,128)S(1)} %get-tuple-element.841), channel_id=1, source_target_pairs={{6,0},{7,1},{0,2},{1,3},{2,4},{3,5},{4,6},{5,7},{14,8},{15,9},{8,1... | collective-permute-start | bytes 98312 | tf_op jit(solution)/shard_map/ppermute | solution.py:18
  319.2 13.9 %collective-permute-start.21 = (f32[64,128]{0,1:T(8,128)S(1)}, f32[64,128]{0,1:T(8,128)S(1)}, u32[]{:S(2)}, u32[]{:S(2)}) collective-permute-start(f32[64,128]{0,1:T(8,128)S(1)} %get-tuple-element.840), channel_id=1, source_target_pairs={{2,0},{3,1},{4,2},{5,3},{6,4},{7,5},{0,6},{1,7},{10,8},{11,9},{12,... | collective-permute-start | bytes 98312 | tf_op jit(solution)/shard_map/ppermute | solution.py:18
  323.0 10.7 %collective-permute-start.22 = (f32[64,128]{0,1:T(8,128)S(1)}, f32[64,128]{0,1:T(8,128)S(1)}, u32[]{:S(2)}, u32[]{:S(2)}) collective-permute-start(f32[64,128]{0,1:T(8,128)S(1)} %get-tuple-element.839), channel_id=1, source_target_pairs={{5,0},{6,1},{7,2},{0,3},{1,4},{2,5},{3,6},{4,7},{13,8},{14,9},{15,... | collective-permute-start | bytes 98312 | tf_op jit(solution)/shard_map/ppermute | solution.py:18
  324.7 10.2 %copy-start.42 = (f32[64,1]{0,1:T(1,128)S(1)}, f32[64,1]{0,1:T(1,128)}, u32[]{:S(2)}) copy-start(f32[64,1]{0,1:T(1,128)} %copy-done.41) | copy-start | bytes 772
  328.6 5.8 collective-permute-start.23
  341.5 17.1 %copy-start.11 = (f32[32,3072]{1,0:T(8,128)S(1)}, f32[32,3072]{1,0:T(8,128)}, u32[]{:S(2)}) copy-start(f32[32,3072]{1,0:T(8,128)} %param.48) | copy-start | bytes 1179652
  341.5 17.1 %copy-start.24 = (f32[3072]{0:T(1024)S(1)}, f32[3072]{0:T(1024)}, u32[]{:S(2)}) copy-start(f32[3072]{0:T(1024)} %param.49) | copy-start | bytes 36868
  383.0 10.8 %copy-start.13 = (f32[8,384]{1,0:T(8,128)S(1)}, f32[8,384]{1,0:T(8,128)}, u32[]{:S(2)}) copy-start(f32[8,384]{1,0:T(8,128)} %mul.242) | copy-start | bytes 36868
  426.5 12.2 %collective-permute-start.24 = (f32[32,128]{1,0:T(8,128)S(1)}, f32[32,128]{1,0:T(8,128)}, u32[]{:S(2)}, u32[]{:S(2)}) collective-permute-start(f32[32,128]{1,0:T(8,128)S(1)} %bitcast.326), channel_id=1, source_target_pairs={{7,0},{0,1},{1,2},{2,3},{3,4},{4,5},{5,6},{6,7},{15,8},{8,9},{9,10... | collective-permute-start | bytes 49160 | tf_op jit(solution)/shard_map/ppermute | solution.py:18
  427.2 14.8 %collective-permute-start.25 = (f32[32,128]{1,0:T(8,128)S(1)}, f32[32,128]{1,0:T(8,128)}, u32[]{:S(2)}, u32[]{:S(2)}) collective-permute-start(f32[32,128]{1,0:T(8,128)S(1)} %bitcast.322), channel_id=1, source_target_pairs={{1,0},{2,1},{3,2},{4,3},{5,4},{6,5},{7,6},{0,7},{9,8},{10,9},{11,1... | collective-permute-start | bytes 49160 | tf_op jit(solution)/shard_map/ppermute | solution.py:18
  430.7 12.0 %collective-permute-start.26 = (f32[32,128]{1,0:T(8,128)S(1)}, f32[32,128]{1,0:T(8,128)}, u32[]{:S(2)}, u32[]{:S(2)}) collective-permute-start(f32[32,128]{1,0:T(8,128)S(1)} %bitcast.318), channel_id=1, source_target_pairs={{6,0},{7,1},{0,2},{1,3},{2,4},{3,5},{4,6},{5,7},{14,8},{15,9},{8,1... | collective-permute-start | bytes 49160 | tf_op jit(solution)/shard_map/ppermute | solution.py:18
  430.7 12.7 %collective-permute-start.27 = (f32[32,128]{1,0:T(8,128)S(1)}, f32[32,128]{1,0:T(8,128)S(1)}, u32[]{:S(2)}, u32[]{:S(2)}) collective-permute-start(f32[32,128]{1,0:T(8,128)S(1)} %bitcast.314), channel_id=1, source_target_pairs={{2,0},{3,1},{4,2},{5,3},{6,4},{7,5},{0,6},{1,7},{10,8},{11,9},{12,... | collective-permute-start | bytes 49160 | tf_op jit(solution)/shard_map/ppermute | solution.py:18
  434.6 8.9 %collective-permute-start.28 = (f32[32,128]{1,0:T(8,128)S(1)}, f32[32,128]{1,0:T(8,128)S(1)}, u32[]{:S(2)}, u32[]{:S(2)}) collective-permute-start(f32[32,128]{1,0:T(8,128)S(1)} %bitcast.310), channel_id=1, source_target_pairs={{5,0},{6,1},{7,2},{0,3},{1,4},{2,5},{3,6},{4,7},{13,8},{14,9},{15,... | collective-permute-start | bytes 49160 | tf_op jit(solution)/shard_map/ppermute | solution.py:18
  435.1 6.2 %copy-start.23 = (f32[32,1793]{1,0:T(8,128)S(1)}, f32[32,1793]{1,0:T(8,128)}, u32[]{:S(2)}) copy-start(f32[32,1793]{1,0:T(8,128)} %constant_dynamic-update-slice_fusion.35) | copy-start | bytes 688516
  438.6 4.8 collective-permute-start.29
  467.0 7.0 %copy-start.1 = (f32[32,1024]{0,1:T(8,128)S(1)}, f32[32,1024]{0,1:T(8,128)}, u32[]{:S(2)}) copy-start(f32[32,1024]{0,1:T(8,128)} %copy-done) | copy-start | bytes 393220
  467.0 7.0 %copy-start.2 = (f32[32,1024]{0,1:T(8,128)S(1)}, f32[32,1024]{0,1:T(8,128)}, u32[]{:S(2)}) copy-start(f32[32,1024]{0,1:T(8,128)} %get-tuple-element.825) | copy-start | bytes 393220
  467.0 7.0 %copy-start.8 = (f32[32,1024]{0,1:T(8,128)S(1)}, f32[32,1024]{0,1:T(8,128)}, u32[]{:S(2)}) copy-start(f32[32,1024]{0,1:T(8,128)} %copy.276) | copy-start | bytes 393220
  467.0 7.0 %copy-start.34 = (f32[32]{0:T(128)S(1)}, f32[32]{0:T(128)}, u32[]{:S(2)}) copy-start(f32[32]{0:T(128)} %copy-done.32) | copy-start | bytes 388
  475.7 13.0 %collective-permute-start.30 = (f32[32,128]{1,0:T(8,128)S(1)}, f32[32,128]{1,0:T(8,128)S(1)}, u32[]{:S(2)}, u32[]{:S(2)}) collective-permute-start(f32[32,128]{1,0:T(8,128)S(1)} %bitcast.328), channel_id=1, source_target_pairs={{7,0},{0,1},{1,2},{2,3},{3,4},{4,5},{5,6},{6,7},{15,8},{8,9},{9,10... | collective-permute-start | bytes 49160 | tf_op jit(solution)/shard_map/ppermute | solution.py:18
  475.8 15.8 %collective-permute-start.31 = (f32[32,128]{1,0:T(8,128)S(1)}, f32[32,128]{1,0:T(8,128)S(1)}, u32[]{:S(2)}, u32[]{:S(2)}) collective-permute-start(f32[32,128]{1,0:T(8,128)S(1)} %bitcast.324), channel_id=1, source_target_pairs={{1,0},{2,1},{3,2},{4,3},{5,4},{6,5},{7,6},{0,7},{9,8},{10,9},{11,1... | collective-permute-start | bytes 49160 | tf_op jit(solution)/shard_map/ppermute | solution.py:18
  479.4 12.2 %collective-permute-start.32 = (f32[32,128]{1,0:T(8,128)S(1)}, f32[32,128]{1,0:T(8,128)S(1)}, u32[]{:S(2)}, u32[]{:S(2)}) collective-permute-start(f32[32,128]{1,0:T(8,128)S(1)} %bitcast.321), channel_id=1, source_target_pairs={{6,0},{7,1},{0,2},{1,3},{2,4},{3,5},{4,6},{5,7},{14,8},{15,9},{8,1... | collective-permute-start | bytes 49160 | tf_op jit(solution)/shard_map/ppermute | solution.py:18
  479.4 12.2 %collective-permute-start.33 = (f32[32,128]{1,0:T(8,128)S(1)}, f32[32,128]{1,0:T(8,128)S(1)}, u32[]{:S(2)}, u32[]{:S(2)}) collective-permute-start(f32[32,128]{1,0:T(8,128)S(1)} %bitcast.317), channel_id=1, source_target_pairs={{2,0},{3,1},{4,2},{5,3},{6,4},{7,5},{0,6},{1,7},{10,8},{11,9},{12,... | collective-permute-start | bytes 49160 | tf_op jit(solution)/shard_map/ppermute | solution.py:18
  483.2 8.4 %collective-permute-start.34 = (f32[32,128]{1,0:T(8,128)S(1)}, f32[32,128]{1,0:T(8,128)S(1)}, u32[]{:S(2)}, u32[]{:S(2)}) collective-permute-start(f32[32,128]{1,0:T(8,128)S(1)} %bitcast.313), channel_id=1, source_target_pairs={{5,0},{6,1},{7,2},{0,3},{1,4},{2,5},{3,6},{4,7},{13,8},{14,9},{15,... | collective-permute-start | bytes 49160 | tf_op jit(solution)/shard_map/ppermute | solution.py:18
  488.7 4.3 collective-permute-start.35
  534.1 7.0 %copy-start.3 = (f32[32,1024]{0,1:T(8,128)S(1)}, f32[32,1024]{0,1:T(8,128)}, u32[]{:S(2)}) copy-start(f32[32,1024]{0,1:T(8,128)} %get-tuple-element.825) | copy-start | bytes 393220
  534.1 7.0 %copy-start.6 = (f32[32,1024]{0,1:T(8,128)S(1)}, f32[32,1024]{0,1:T(8,128)}, u32[]{:S(2)}) copy-start(f32[32,1024]{0,1:T(8,128)} %copy.280) | copy-start | bytes 393220
  534.1 7.0 %copy-start.22 = (pred[1024]{0:T(1024)(128)(4,1)S(1)}, pred[1024]{0:T(1024)(128)(4,1)}, u32[]{:S(2)}) copy-start(pred[1024]{0:T(1024)(128)(4,1)} %iota_compare_fusion.87) | copy-start | bytes 3076
  534.1 7.0 %copy-start.27 = (f32[1024]{0:T(1024)S(1)}, f32[1024]{0:T(1024)}, u32[]{:S(2)}) copy-start(f32[1024]{0:T(1024)} %get-tuple-element.877) | copy-start | bytes 12292
  (16 other events, 51.2 us)
Sparse Core Ops, SparseCore 0:
  557.9 44.0 all-reduce.6
where the time goes:
time: 621 us; the launch traced here: 611 us
  matrix products  185 us (30%)
  local copies, waits for them, and re-layouts  175 us (28%)
  other arithmetic  93.5 us (15%)
  starting transfers between devices  62.6 us (10%)
  waiting for transfers between devices  46 us (7%)
  blocking collectives  29 us (5%)
  between operations  17.2 us (3%)
    dot_general x132, matrix products, exact_dot(): jnp.dot(left_side, right_side, precision=lax.Precision.HIGHEST, preferred...  179 us
    ppermute x36, starting transfers between devices, passed_along(): return lax.ppermute(block, axis, route)  62.6 us
    reduce_sum x8, other arithmetic, divergence(): outgoing = jnp.sum(fluxes.reshape(levels, cell_count, 3), axis=2)  50.5 us
    psum x1, waiting for transfers between devices, per_device(): ensemble = lax.psum(current, 'member') / lax.axis_size('member')  43.2 us
    unnamed x140, local copies, waits for them, and re-layouts  39.7 us
    reshape x10, local copies, waits for them, and re-layouts, starts_of(): jnp.broadcast_to(fields[:, :, None], (levels, cell_count, 3))  31.1 us
    psum x2, blocking collectives, per_device(): lax.psum((jnp.sum(current * cell_area[None, :], axis=1), jnp.sum(cell_are...  29 us
    transpose x6, other arithmetic, divergence(): jnp.transpose(fluxes.reshape(levels, block_count, block_size), (1, 0, 2))  19.8 us
  transfers between devices with their start and end apart: 37, of which 3 were waited for; matrix products, arithmetic and copies ran while one was open for 12% of the time, Pallas kernels for 0%

commit v1 on v0

v1 whole, which is shorter than its diff:
```python
import functools

import jax
import jax.numpy as jnp
from jax import lax
from jax.experimental import pallas as pl
from jax.experimental.pallas import tpu as pltpu
from jax.sharding import PartitionSpec as P

STEPS = 2
NS = 3
TIME_STEP = 0.25
LANES = 128
MESH = pl.DeviceIdType.MESH
F32 = jnp.float32
BF16 = jnp.bfloat16


def neighbour_offsets(count):
    return [(b // 2 + 1) * (1 - 2 * (b % 2)) for b in range(count)]


def mm(a, b):
    return jnp.dot(a, b, preferred_element_type=F32)


def mm_nt(a, b):
    return lax.dot_general(a, b, (((1,), (1,)), ((), ())), preferred_element_type=F32)


def halves(x):
    high = x.astype(BF16)
    low = (x - high.astype(F32)).astype(BF16)
    return jnp.concatenate([high, low], axis=0)


def fold(x):
    rows = x.shape[0] // 2
    return x[:rows] + x[rows:]


def kernel(
    n,
    members,
    p_ref,
    q_ref,
    t_ref,
    par_ref,
    v_ref,
    ext_ref,
    met_ref,
    inv_ref,
    own_ref,
    exp_ref,
    fin_ref,
    p_out,
    t_out,
    e_out,
    pick,
    g,
    a_hi,
    a_lo,
    b_loc,
    diag,
    xv,
    vj,
    ej,
    send,
    recv,
    mean_send,
    mean_recv,
    mem_send,
    mem_recv,
    mm_send,
    mm_recv,
    send_sem,
    recv_sem,
    mean_ssem,
    mean_rsem,
    mem_ssem,
    mem_rsem,
    mm_ssem,
    mm_rsem,
):
    levels, cells = p_ref.shape[1], p_ref.shape[2]
    slabs = v_ref.shape[1] // cells
    blocks = cells // LANES
    wide = slabs * LANES
    nb = exp_ref.shape[1]
    hb = exp_ref.shape[2]
    halo = nb * hb
    me = lax.axis_index("dom")
    mine = lax.axis_index("member")
    offsets = neighbour_offsets(nb)
    stages = members.bit_length() - 1

    def dom_peer(k):
        return {"dom": lax.rem(me + (k % n), n)}

    def member_peer(stage):
        bit = 1 << stage
        return {"member": mine + bit - 2 * bit * lax.rem(mine // bit, 2)}

    barrier = pltpu.get_barrier_semaphore()
    for k in range(1, n):
        pl.semaphore_signal(barrier, inc=1, device_id=dom_peer(k), device_id_type=MESH)
    for s in range(stages):
        pl.semaphore_signal(barrier, inc=1, device_id=member_peer(s), device_id_type=MESH)

    speed = par_ref[0, 0]
    kappa = 0.5 * par_ref[0, 1]
    mixing = 0.6 * par_ref[0, 2]
    couple = par_ref[0, 3]
    inverse = inv_ref[...]
    owned = lax.broadcasted_iota(jnp.int32, (1, cells), 1) < own_ref[0]
    area = jnp.where(owned, 1.0 / inverse, 0.0)
    started = []

    strip = 16
    sub = lax.broadcasted_iota(jnp.int32, (strip, 1), 0)
    for b in range(nb):
        row = exp_ref[0, b : b + 1, :]

        def build_pick(s, carry, row=row, b=b):
            rows = lax.broadcasted_iota(jnp.int32, (strip, hb), 0) + s * strip
            pick[pl.ds(pl.multiple_of(s * strip, strip), strip), b * hb : (b + 1) * hb] = (
                jnp.where(rows == row, 1.0, 0.0).astype(BF16)
            )
            return carry

        lax.fori_loop(0, cells // strip, build_pick, 0)

    def exchange(slot, chosen):
        copies = []
        for b, offset in enumerate(offsets):
            send[slot, b] = chosen[:, b * hb : (b + 1) * hb]
            copy = pltpu.make_async_remote_copy(
                src_ref=send.at[slot, b],
                dst_ref=recv.at[slot, b],
                send_sem=send_sem.at[slot, b],
                recv_sem=recv_sem.at[slot, b],
                device_id=dom_peer(offset),
                device_id_type=MESH,
            )
            copy.start()
            copies.append(copy)
        started.extend(copies)
        return copies

    def arrived(slot, copies):
        for copy in copies:
            copy.wait_recv()
        return halves(jnp.concatenate([recv[slot, b] for b in range(nb)], axis=1))

    current = p_ref[0]
    previous = q_ref[0]
    theta = t_ref[0]
    xp = halves(current)
    xt = halves(theta)
    both = mm(jnp.concatenate([xt, xp], axis=0), pick[...])
    pl.semaphore_wait(barrier, n - 1 + stages)
    t_copies = exchange(0, fold(both[: 2 * levels]))
    p_copies = exchange(1, fold(both[2 * levels :]))

    base = levels * blocks
    for b in range(blocks):
        cut = slice(b * wide, (b + 1) * wide)
        xv[b * levels : (b + 1) * levels, :] = v_ref[:, cut]
        ends = fin_ref[1:2, cut]
        xv[base + b : base + b + 1, :] = ext_ref[:, cut]
        xv[base + blocks + b : base + blocks + b + 1, :] = met_ref[:, cut]
        xv[base + 2 * blocks + b : base + 2 * blocks + b + 1, :] = (ends // 8).astype(F32)
        xv[base + 3 * blocks + b : base + 3 * blocks + b + 1, :] = (ends % 8).astype(F32)
    ri = lax.broadcasted_iota(jnp.int32, (wide, wide), 0)
    ci = lax.broadcasted_iota(jnp.int32, (wide, wide), 1)
    order = jnp.where(ri == slabs * (ci % LANES) + ci // LANES, 1.0, 0.0).astype(BF16)
    for b in range(blocks):
        y = fold(mm(halves(xv[b * levels : (b + 1) * levels, :]), order))
        for j in range(slabs):
            vj[j, :, b * LANES : (b + 1) * LANES] = y[:, j * LANES : (j + 1) * LANES]
    y = fold(mm(halves(xv[base : base + 4 * blocks, :]), order))
    for kind in range(4):
        for j in range(slabs):
            for b in range(blocks):
                ej[kind * slabs + j : kind * slabs + j + 1, b * LANES : (b + 1) * LANES] = y[
                    kind * blocks + b : kind * blocks + b + 1, j * LANES : (j + 1) * LANES
                ]
    extent = [ej[j : j + 1, :] for j in range(slabs)]
    metric = [ej[slabs + j : slabs + j + 1, :] for j in range(slabs)]
    ends = [
        8.0 * ej[2 * slabs + j : 2 * slabs + j + 1, :] + ej[3 * slabs + j : 3 * slabs + j + 1, :]
        for j in range(slabs)
    ]

    def strip_of(s):
        at = pl.ds(pl.multiple_of(s * strip, strip), strip)
        rows = (lax.broadcasted_iota(jnp.int32, (strip, cells), 0) + s * strip).astype(F32)
        total = jnp.zeros((strip, cells), F32)
        for j in range(slabs):
            hit = rows == ends[j]
            g[at, j * cells : (j + 1) * cells] = jnp.where(hit, 1.0, 0.0).astype(BF16)
            total = total + jnp.where(hit, metric[j], 0.0)
        return at, total

    def put(at, value, columns):
        high = value.astype(BF16)
        a_hi[at, columns] = high
        a_lo[at, columns] = (value - high.astype(F32)).astype(BF16)

    def build_local(s, carry):
        at, total = strip_of(s)
        b_loc[at, :] = total
        return carry

    def build_halo(s, carry):
        at, total = strip_of(s)
        put(at, total, slice(None))
        diag[...] += total
        return carry

    diag[...] = jnp.zeros_like(diag)
    lax.fori_loop(0, cells // strip, build_local, 0)
    lax.fori_loop(cells // strip, (cells + halo) // strip, build_halo, 0)

    def symmetric(i, carry):
        at = pl.ds(pl.multiple_of(i * LANES, LANES), LANES)
        for j in range(blocks):
            cut = slice(j * LANES, (j + 1) * LANES)
            value = b_loc[at, cut] + b_loc[cut, at].T
            put(at, value, cut)
            total = value[:strip]
            for r in range(1, LANES // strip):
                total = total + value[r * strip : (r + 1) * strip]
            diag[:, cut] += total
        return carry

    lax.fori_loop(0, blocks, symmetric, 0)
    degree = jnp.sum(diag[...], axis=0, keepdims=True)
    scale = speed * inverse

    def far_local(x, j):
        return fold(mm(x, g[:cells, j * cells : (j + 1) * cells]))

    def far_halo(x, j):
        return fold(mm(x, g[cells:, j * cells : (j + 1) * cells]))

    def slab_flux(theta, far, j):
        wind = vj[j]
        flux = extent[j] * (
            0.5 * wind * (theta + far) - (0.5 * jnp.abs(wind) + kappa) * (far - theta)
        )
        incoming = mm_nt(halves(flux), g[:cells, j * cells : (j + 1) * cells])
        return flux - fold(incoming)

    def theta_end(theta, div):
        step = theta[1:] - theta[:-1]
        zero = jnp.zeros((1, cells), F32)
        vertical = mixing * (
            jnp.concatenate([step, zero], 0) - jnp.concatenate([zero, step], 0)
        )
        advanced = jnp.where(owned, theta + TIME_STEP * (vertical - inverse * div), theta)
        return advanced, couple * (advanced - theta) / NS

    def local_part(x):
        return fold(mm(x, a_hi[:cells, :])) + mm(x[:levels], a_lo[:cells, :])

    def halo_part(x):
        return fold(mm(x, a_hi[cells:, :])) + mm(x[:levels], a_lo[cells:, :])

    def partial_mean(slot, field):
        weighted = jnp.sum(field * area, axis=1, keepdims=True)
        whole = jnp.sum(area, axis=1, keepdims=True)
        row_at = lax.broadcasted_iota(jnp.int32, (levels, LANES), 0)
        lane_at = lax.broadcasted_iota(jnp.int32, (levels, LANES), 1)
        row = jnp.sum(jnp.where(row_at == lane_at, weighted, 0.0), axis=0, keepdims=True)
        lane = lax.broadcasted_iota(jnp.int32, (1, LANES), 1)
        row = jnp.where(lane < levels, row, whole)
        mean_send[slot] = jnp.broadcast_to(row, (8, LANES))
        copies = []
        for k in range(1, n):
            copy = pltpu.make_async_remote_copy(
                src_ref=mean_send.at[slot],
                dst_ref=mean_recv.at[slot, k - 1],
                send_sem=mean_ssem.at[slot, k - 1],
                recv_sem=mean_rsem.at[slot, k - 1],
                device_id=dom_peer(k),
                device_id_type=MESH,
            )
            copy.start()
            copies.append(copy)
        started.extend(copies)
        return copies

    def mean_row(slot, copies):
        total = mean_send[slot]
        for k, copy in enumerate(copies):
            copy.wait_recv()
            total = total + mean_recv[slot, k]
        return total / total[:, levels : levels + 1]

    def as_column(row):
        row_at = lax.broadcasted_iota(jnp.int32, (levels, LANES), 0)
        lane_at = lax.broadcasted_iota(jnp.int32, (levels, LANES), 1)
        return jnp.sum(jnp.where(row_at == lane_at, row[0:1], 0.0), axis=1, keepdims=True)

    ht = arrived(0, t_copies)
    div = jnp.zeros((levels, cells), F32)
    for j in range(slabs):
        div = div + slab_flux(theta, far_local(xt, j) + far_halo(ht, j), j)
    theta1, forcing = theta_end(theta, div)
    xt1 = halves(theta1)

    mean_copies = None
    slot = 1
    total_substeps = STEPS * NS
    div = jnp.zeros((levels, cells), F32)
    ht1 = None
    for k in range(total_substeps):
        accel = local_part(xp) - degree * current
        if k == NS - 1:
            ht1 = arrived(0 + STEPS * NS + 1, t_copies)
            for j in range(slabs - 1):
                div = div + slab_flux(theta1, far_local(xt1, j) + far_halo(ht1, j), j)
        if k == NS:
            mean_copies = partial_mean(0, current)
            j = slabs - 1
            div = div + slab_flux(theta1, far_local(xt1, j) + far_halo(ht1, j), j)
            theta2, forcing = theta_end(theta1, div)
            t_out[0] = theta2
        accel = accel + halo_part(arrived(slot, p_copies))
        stepped = jnp.where(
            owned, 2.0 * current - previous + scale * accel + forcing, current
        )
        previous, current = current, stepped
        if k < total_substeps - 1:
            slot += 1
            xp = halves(current)
            p_copies = exchange(slot, fold(mm(xp, pick[...])))
            if k == 0:
                t_copies = exchange(STEPS * NS + 1, fold(mm(xt1, pick[...])))

    first = as_column(mean_row(0, mean_copies))
    current = jnp.where(owned, current - first, current)

    width = cells // max(stages, 1)
    last_copies = partial_mean(1, current)
    e_out[...] = current

    def member_stage(stage):
        copies = []
        for c in range(stages):
            cut = slice(c * width, (c + 1) * width)
            mem_send[stage, c] = e_out[:, cut]
            copy = pltpu.make_async_remote_copy(
                src_ref=mem_send.at[stage, c],
                dst_ref=mem_recv.at[stage, c],
                send_sem=mem_ssem.at[stage, c],
                recv_sem=mem_rsem.at[stage, c],
                device_id=member_peer((stage + c) % stages),
                device_id_type=MESH,
            )
            copy.start()
            copies.append(copy)
        started.extend(copies)
        return copies

    def member_add(stage, copies):
        for c, copy in enumerate(copies):
            cut = slice(c * width, (c + 1) * width)
            copy.wait_recv()
            e_out[:, cut] = mem_send[stage, c] + mem_recv[stage, c]

    bulk = member_stage(0) if stages else []
    last = mean_row(1, last_copies)
    summed = last
    p_out[0] = jnp.where(owned, current - as_column(last), current)
    for s in range(stages):
        mm_send[s] = summed
        copy = pltpu.make_async_remote_copy(
            src_ref=mm_send.at[s],
            dst_ref=mm_recv.at[s],
            send_sem=mm_ssem.at[s],
            recv_sem=mm_rsem.at[s],
            device_id=member_peer(s),
            device_id_type=MESH,
        )
        copy.start()
        started.append(copy)
        member_add(s, bulk)
        if s + 1 < stages:
            bulk = member_stage(s + 1)
        copy.wait_recv()
        summed = mm_send[s] + mm_recv[s]
    e_out[...] = (e_out[...] - jnp.where(owned, as_column(summed), 0.0)) / members
    for copy in started:
        copy.wait_send()


def solution(mesh):
    n = mesh.shape["dom"]
    members = mesh.shape["member"]

    def per_device(
        acoustic_perturbation,
        prior_acoustic_state,
        thermal_anomaly,
        model_parameters,
        crossing_velocity,
        face_extent,
        face_metric_factor,
        reciprocal_polygon_surface,
        owned_totals,
        export_lists,
        face_neighbour_pair,
        polygon_side_lookup,
    ):
        _, levels, cells = acoustic_perturbation.shape
        edges = face_extent.shape[0]
        slabs = edges // cells
        blocks = cells // LANES
        nb, hb = export_lists.shape[1:]
        halo = nb * hb
        stages = members.bit_length() - 1
        some = max(stages, 1)
        slots = STEPS * NS + 2
        vmem = pl.BlockSpec(memory_space=pltpu.VMEM)
        smem = pl.BlockSpec(memory_space=pltpu.SMEM)
        dma = pltpu.SemaphoreType.DMA
        return pl.pallas_call(
            functools.partial(kernel, n, members),
            out_shape=(
                jax.ShapeDtypeStruct((1, levels, cells), F32),
                jax.ShapeDtypeStruct((1, levels, cells), F32),
                jax.ShapeDtypeStruct((levels, cells), F32),
            ),
            in_specs=[vmem, vmem, vmem, smem, vmem, vmem, vmem, vmem, smem, vmem, vmem],
            out_specs=(vmem, vmem, vmem),
            scratch_shapes=[
                pltpu.VMEM((cells, halo), BF16),
                pltpu.VMEM((cells + halo, edges), BF16),
                pltpu.VMEM((cells + halo, cells), BF16),
                pltpu.VMEM((cells + halo, cells), BF16),
                pltpu.VMEM((cells, cells), F32),
                pltpu.VMEM((16, cells), F32),
                pltpu.VMEM((levels * blocks + 4 * blocks, slabs * LANES), F32),
                pltpu.VMEM((slabs, levels, cells), F32),
                pltpu.VMEM((16, cells), F32),
                pltpu.VMEM((slots, nb, levels, hb), F32),
                pltpu.VMEM((slots, nb, levels, hb), F32),
                pltpu.VMEM((STEPS, 8, LANES), F32),
                pltpu.VMEM((STEPS, n - 1, 8, LANES), F32),
                pltpu.VMEM((some, some, levels, cells // some), F32),
                pltpu.VMEM((some, some, levels, cells // some), F32),
                pltpu.VMEM((some, 8, LANES), F32),
                pltpu.VMEM((some, 8, LANES), F32),
                dma((slots, nb)),
                dma((slots, nb)),
                dma((STEPS, n - 1)),
                dma((STEPS, n - 1)),
                dma((some, some)),
                dma((some, some)),
                dma((some,)),
                dma((some,)),
            ],
            compiler_params=pltpu.CompilerParams(
                collective_id=0, has_side_effects=True, vmem_limit_bytes=60 * 1024 * 1024
            ),
        )(
            acoustic_perturbation,
            prior_acoustic_state,
            thermal_anomaly,
            model_parameters,
            crossing_velocity,
            face_extent[None],
            face_metric_factor[None],
            reciprocal_polygon_surface[None],
            owned_totals,
            export_lists,
            face_neighbour_pair,
        )

    in_specs = (
        P("member", None, "dom"),
        P("member", None, "dom"),
        P("member", None, "dom"),
        P("member", None),
        P(None, "dom"),
        P("dom"),
        P("dom"),
        P("dom"),
        P("dom"),
        P("dom", None, None),
        P(None, "dom"),
        P(None, "dom"),
    )
    out_specs = (P("member", None, "dom"), P("member", None, "dom"), P(None, "dom"))
    return jax.shard_map(
        per_device, mesh=mesh, in_specs=in_specs, out_specs=out_specs, check_vma=False
    )
```

time: 621 us -> 63.7 us (0.10); the launches traced: 611 us -> 63.5 us
  matrix products: 185 us -> 0 us
  local copies, waits for them, and re-layouts: 175 us -> 4.48 us
  other arithmetic: 93.5 us -> 0 us
  starting transfers between devices: 62.6 us -> 0 us
  Pallas kernels: 0 us -> 57.7 us
  waiting for transfers between devices: 46 us -> 0 us
  blocking collectives: 29 us -> 0 us
  between operations: 17.2 us -> 1.3 us
    dot_general x132 -> x0, matrix products: 179 us -> none  [exact_dot(): jnp.dot(left_side, right_side, precision=lax.Precision.HIGHEST, preferred...]
    ppermute x36 -> x0, starting transfers between devices: 62.6 us -> none  [passed_along(): return lax.ppermute(block, axis, route)]
    pallas_call x0 -> x1, Pallas kernels: none -> 57.7 us  [per_device(): pl.pallas_call(functools.partial(kernel, n, members), out_shape=(jax.Shap...]
    reshape x24 -> x0, local copies, waits for them, and re-layouts: 54.7 us -> none  [the longest x10 31.1 us: starts_of(): jnp.broadcast_to(fields[:, :, None], (levels, cell_count, 3))]
    reduce_sum x10 -> x0, other arithmetic: 52.3 us -> none  [the longest x8 50.5 us: divergence(): outgoing = jnp.sum(fluxes.reshape(levels, cell_count, 3), axis=2)]
    psum x1 -> x0, waiting for transfers between devices: 43.2 us -> none  [per_device(): ensemble = lax.psum(current, 'member') / lax.axis_size('member')]
    unnamed x140 -> x10, local copies, waits for them, and re-layouts: 39.7 us -> 4.48 us
    psum x2 -> x0, blocking collectives: 29 us -> none  [per_device(): lax.psum((jnp.sum(current * cell_area[None, :], axis=1), jnp.sum(cell_are...]
  transfers between devices with their start and end apart: 37 -> 0, of which waited for: 3 -> 0; matrix products, arithmetic and copies ran while one was open for 12% -> 0% of each run, Pallas kernels for 0% -> 0%
where the time goes in v1:
time: 63.7 us; the launch traced here: 63.5 us
  Pallas kernels  57.7 us (91%)
  local copies, waits for them, and re-layouts  4.48 us (7%)
  between operations  1.3 us (2%)
    pallas_call x1, Pallas kernels, per_device(): pl.pallas_call(functools.partial(kernel, n, members), out_shape=(jax.Shap...  57.7 us
    unnamed x10, local copies, waits for them, and re-layouts  4.48 us

profile of v1, /device:TPU:0, one launch (start us, length us, event | category | flops | bytes accessed | tf_op | source)
XLA Modules:
  0.0 63.5 jit_solution(1622990878739127110)
XLA Ops:
  1.3 0.0 copy-start.2
  1.3 0.7 %copy-done.2 = s32[1,6,128]{2,0,1:T(1,128)S(1)} copy-done((s32[1,6,128]{2,0,1:T(1,128)S(1)}, s32[1,6,128]{2,0,1:T(1,128)}, u32[]{:S(2)}) %copy-start.2) | copy-done | bytes 3096
  2.0 0.6 copy.14.exp_ref
  2.6 57.7 %shard_map.130 = (f32[1,32,1024]{2,1,0:T(8,128)}, f32[1,32,1024]{2,1,0:T(8,128)}, f32[32,1024]{1,0:T(8,128)}) custom-call(f32[1,32,1024]{2,1,0:T(8,128)} %p_ref.1, f32[1,32,1024]{2,1,0:T(8,128)} %q_ref.1, f32[1,32,1024]{2,1,0:T(8,128)} %t_ref.1, f32[1,4]{1,0:T(1,128)} %par_ref.1, f32[32,3072]{1,0:T(8,128)} %v_ref.1, f32[1,3072]{1,0:T(1,128)} %bitcast.3, ...), custom_call_target="tpu_custom_call" | custom-call | tf_op jit(solution)/shard_map/pallas_call | solution.py:429
  60.2 0.0 copy-start.1
  60.2 1.6 %copy.19 = f32[1,32,1024]{2,1,0:T(8,128)} copy(f32[1,32,1024]{2,1,0:T(8,128)} %get-tuple-element.6) | data formatting | bytes 262144
  61.8 0.0 copy-done.1
  61.8 0.0 copy-start
  61.8 0.7 %copy.20 = f32[1,32,1024]{2,1,0:T(8,128)} copy(f32[1,32,1024]{2,1,0:T(8,128)S(1)} %copy-done.1) | data formatting | bytes 262144
  62.5 0.3 copy-done
  62.8 0.7 %copy.21 = f32[32,1024]{1,0:T(8,128)} copy(f32[32,1024]{1,0:T(8,128)S(1)} %copy-done) | data formatting | bytes 262144
Async XLA Ops:
  1.3 0.7 %copy-start.2 = (s32[1,6,128]{2,0,1:T(1,128)S(1)}, s32[1,6,128]{2,0,1:T(1,128)}, u32[]{:S(2)}) copy-start(s32[1,6,128]{2,0,1:T(1,128)} %param.21) | copy-start | bytes 9220
  60.2 1.6 %copy-start.1 = (f32[1,32,1024]{2,1,0:T(8,128)S(1)}, f32[1,32,1024]{2,1,0:T(8,128)}, u32[]{:S(2)}) copy-start(f32[1,32,1024]{2,1,0:T(8,128)} %get-tuple-element.7) | copy-start | bytes 393220
  61.8 1.0 %copy-start = (f32[32,1024]{1,0:T(8,128)S(1)}, f32[32,1024]{1,0:T(8,128)}, u32[]{:S(2)}) copy-start(f32[32,1024]{1,0:T(8,128)} %get-tuple-element.8) | copy-start | bytes 393220
